TPU v7x, 32 devices: a whole 2x2x4 slice. The times are simulated.
32 devices in a mesh: strip: 8 (over z, x), col: 4 (over y, core).
Axes of the slice: x: 2, y: 2, z: 4, core: 2. Of those that a mesh axis runs over, the one named last changes fastest.
Arguments:
- residuals: float32 [16, 64, 2560], P('strip'), may hold values from -6 to 6
- corr_rows: float32 [64], replicated, may hold values from 0.5 to 2
- corr_cols: float32 [2560], replicated, may hold values from 0.5 to 2
- row_anchor: int32 [16], replicated, may hold values from 0 to 64
- col_anchor: int32 [16], replicated, may hold values from 0 to 7680
- valid_first: int32 [16], replicated, may hold values from 0 to 15
- valid_end: int32 [16], replicated, may hold values from 49 to 64
- facet_of_slot: int32 [16], replicated, may hold values from 0 to 15, each once
Outputs:
- stitched: float32 [128, 10240], P('strip', 'col')
- column_power: float32 [10240], P('col')
Inputs may be any that keep to these rules, and one draw needn't show every extreme that they name: facet_of_slot names each of the 16 facets exactly once.
All inputs are finite; a program needn't handle non-finite values.
Results may differ from a plain program's by a relative error of at most 0.0003.
Values sent between devices are 32-bit elements; how exact they have to be, the bound alone decides.
No kernel may reach another device: no remote copies, remote signals or barrier semaphores. Data moves between devices by JAX's collectives and lax.ppermute only.
A program may use at most 64 MiB of HBM per device.

v0:
```python
import jax
import jax.numpy as jnp
from jax import lax
from jax.sharding import PartitionSpec as P


def tapers(count):
    position = (jnp.arange(count).astype(jnp.float32) + 0.5) / count
    return jnp.sin(jnp.pi * position) ** 2


def body(
    residuals, corr_rows, corr_cols, row_anchor, col_anchor, valid_first, valid_end, facet_of_slot
):
    local_count, facet_rows, facet_cols = residuals.shape
    strip_count = lax.axis_size("strip")
    strip_rows = facet_rows // 4
    image_rows = strip_count * strip_rows
    strip_index = lax.axis_index("strip")
    group_index = lax.axis_index("col")
    row_index = jnp.arange(facet_rows)
    row_taper = tapers(facet_rows)
    col_taper = tapers(facet_cols)
    correction = corr_rows[:, None] * corr_cols[None, :]
    side_blank = jnp.zeros((facet_rows, facet_cols), jnp.float32)
    num_bands = []
    for position in range(local_count):
        facet_id = facet_of_slot[strip_index * local_count + position]
        inside = (row_index >= valid_first[facet_id]) & (row_index < valid_end[facet_id])
        row_weight = jnp.where(inside, row_taper, 0.0)
        weight = row_weight[:, None] * col_taper[None, :]
        col_start = jnp.clip(
            group_index * facet_cols - col_anchor[facet_id] + facet_cols, 0, 2 * facet_cols
        )
        padded = jnp.concatenate(
            [side_blank, weight * correction * residuals[position], side_blank], axis=1
        )
        shifted = lax.dynamic_slice_in_dim(padded, col_start, facet_cols, 1)
        canvas = jnp.zeros((image_rows, facet_cols), jnp.float32)
        canvas = lax.dynamic_update_slice(canvas, shifted, (row_anchor[facet_id], 0))
        num_bands.append(canvas.reshape(strip_count, strip_rows, facet_cols))
    num_send = jnp.stack(num_bands, axis=1)
    got_num = lax.all_to_all(num_send, "strip", split_axis=0, concat_axis=0, tiled=True)
    facet_ids = jnp.arange(facet_of_slot.shape[0])
    row_local = strip_index * strip_rows + jnp.arange(strip_rows)
    row_pos = row_local[None, :] - row_anchor[:, None]
    row_inside = (row_pos >= valid_first[:, None]) & (row_pos < valid_end[:, None])
    row_value = jnp.sin(jnp.pi * (row_pos.astype(jnp.float32) + 0.5) / facet_rows) ** 2
    row_part = jnp.where(row_inside, row_value, 0.0)
    col_local = group_index * facet_cols + jnp.arange(facet_cols)
    col_pos = col_local[None, :] - col_anchor[facet_ids][:, None]
    col_inside = (col_pos >= 0) & (col_pos < facet_cols)
    col_value = jnp.sin(jnp.pi * (col_pos.astype(jnp.float32) + 0.5) / facet_cols) ** 2
    col_part = jnp.where(col_inside, col_value, 0.0)
    denominator = jnp.einsum("fv,fu->vu", row_part, col_part, precision=lax.Precision.HIGHEST)
    numerator = jnp.sum(got_num, axis=(0, 1))
    stitched = numerator / jnp.maximum(denominator, 0.5)
    column_sums = lax.psum(jnp.sum(stitched * stitched, axis=0), "strip")
    return (stitched, column_sums / image_rows)


def solution(mesh):
    in_specs = (P("strip", None, None), P(), P(), P(), P(), P(), P(), P())
    out_specs = (P("strip", "col"), P("col"))
    return jax.shard_map(body, mesh=mesh, in_specs=in_specs, out_specs=out_specs, check_vma=False)
```

profile of v0, /device:TPU:0, one launch (start us, length us, event | category | flops | bytes accessed | tf_op | source)
XLA Modules:
  0.0 127.8 jit_solution(10135443065391539872)
XLA Ops:
  0.6 1.3 %fusion.47 = (s32[1]{0:T(128)}, s32[1]{0:T(128)}) fusion(s32[16]{0:T(128)} %param.15, s32[]{:T(128)S(6)} %select_n.50, s32[]{:T(128)S(6)} %select_n.54), kind=kLoop, calls=%fused_computation.69 | loop fusion | bytes 24 | tf_op jit(solution)/shard_map/dynamic_slice | solution.py:28
  4.6 0.1 sine_multiply_fusion
  5.9 1.4 %fusion.43 = (s32[1]{0:T(128)}, s32[1]{0:T(128)}, s32[1]{0:T(128)}, s32[1]{0:T(128)}) fusion(s32[16]{0:T(128)} %param.11, s32[]{:T(128)S(6)} %select_n.51, s32[]{:T(128)S(6)} %select_n.55, s32[16]{0:T(128)} %param.13), kind=kLoop, calls=%fused_computation.65 | loop fusion | bytes 40 | tf_op jit(solution)/shard_map/dynamic_slice | solution.py:40
  9.8 1.4 %fusion.45 = (s32[1]{0:T(128)}, s32[1]{0:T(128)}, s32[1]{0:T(128)}, s32[1]{0:T(128)}) fusion(s32[16]{0:T(128)} %param.14, s32[]{:T(128)S(6)} %select_n.51, s32[]{:T(128)S(6)} %select_n.55, s32[16]{0:T(128)} %param.12), kind=kLoop, calls=%fused_computation.67 | loop fusion | bytes 40 | tf_op jit(solution)/shard_map/dynamic_slice | solution.py:29
  12.5 1.2 and_select_fusion
  13.7 1.4 %and_select_fusion.1 = f32[64]{0:T(128)S(1)} fusion(s32[]{:T(128)} %bitcast.2, s32[]{:T(128)} %bitcast.1), kind=kLoop, calls=%fused_computation.56 | loop fusion | flops 512 | bytes 264 | tf_op jit(solution)/shard_map/jit(_where)/select_n | solution.py:30
  16.3 1.5 %fusion.1 = (f32[64,2560]{1,0:T(8,128)S(1)}, f32[64,2560]{1,0:T(8,128)S(1)}) fusion(f32[2,64,2560]{2,1,0:T(8,128)} %param.8, f32[2560]{0:T(1024)} %param.10, f32[64]{0:T(128)} %param.9, f32[2560]{0:T(1024)S(1)} %sine_multiply_fusion, f32[64]{0:T(128)S(1)} %and_select_fusion.1, f32[64]{0:T(128)S(1)} %and_select_fusion), kind=kLoop, calls=%fused_computation.12 | loop fusion | flops 1146880 | bytes 2642688 | tf_op jit(solution)/shard_map/mul | solution.py:36
  17.9 1.1 fusion.6
  19.0 0.1 broadcast.78.clone.1
  19.2 1.1 dynamic_update_slice.6
  20.3 0.1 broadcast.78.clone
  20.4 1.0 dynamic_update_slice.7
  21.4 1.7 %pad_maximum_fusion = f32[8,2,16,2560]{3,2,1,0:T(8,128)} fusion(f32[8,1,16,2560]{3,2,1,0:T(8,128)S(1)} %bitcast.16, f32[8,1,16,2560]{3,2,1,0:T(8,128)S(1)} %bitcast.17), kind=kLoop, calls=%fused_computation.7 | loop fusion | flops 655360 | bytes 5242880 | tf_op jit(solution)/shard_map/stack | solution.py:42
  23.2 0.0 copy-start
  23.2 7.5 %all-to-all-start = ((f32[8,2,16,2560]{3,2,1,0:T(8,128)}), f32[8,2,16,2560]{3,2,1,0:T(8,128)S(1)}, u32[]{:S(2)}, u32[]{:S(2)}) async-start(f32[8,2,16,2560]{3,2,1,0:T(8,128)} %pad_maximum_fusion), calls=%async_computation | async-start | bytes 5242880 | tf_op jit(solution)/shard_map/all_to_all | solution.py:43
  30.7 0.0 copy-start.1
  30.7 0.0 copy-start.2
  30.7 0.0 copy-start.3
  30.7 0.0 copy-done
  30.8 0.7 gather_fusion
  31.4 58.7 %all-to-all-done = f32[8,2,16,2560]{3,2,1,0:T(8,128)S(1)} async-done(((f32[8,2,16,2560]{3,2,1,0:T(8,128)}), f32[8,2,16,2560]{3,2,1,0:T(8,128)S(1)}, u32[]{:S(2)}, u32[]{:S(2)}) %all-to-all-start) | async-done | bytes 2621472 | tf_op jit(solution)/shard_map/all_to_all | solution.py:43
  90.2 0.1 reduce_sum.18
  90.3 0.0 copy-done.1
  90.3 0.0 copy-done.2
  90.3 0.0 copy-done.3
  90.3 1.6 %multiply_reduce_fusion = (f32[2560]{0:T(1024)S(1)}, f32[16,2560]{1,0:T(8,128)}) fusion(f32[16,2560]{1,0:T(8,128)S(1)} %reduce_sum.18, s32[16]{0:T(128)S(1)} %gather_fusion, s32[2560]{0:T(1024)S(1)} %iota_add_fusion, s32[16]{0:T(128)S(1)} %copy-done.1, s32[16]{0:T(128)S(1)} %copy-done.3, s32[16]{0:T(128)S(1)} %copy-done.2, s32[16]{0:T(128)S(1)} %iota_add_fusion.1), kind=kOutput, calls=%fused_computation.26 | convolution fusion | flops 8396544 | bytes 348480 | tf_op jit(solution)/shard_map/fv,fu->vu/dot_general | solution.py:55
  92.0 35.2 %psum.7 = f32[2560]{0:T(1024)S(1)} all-reduce(f32[2560]{0:T(1024)S(1)} %get-tuple-element.16), channel_id=1, replica_groups=mesh['strip'=8,'col'=4] {'strip'}, use_global_device_ids=true, to_apply=%region_2.3 | all-reduce | flops 2560 | bytes 20480 | tf_op jit(solution)/shard_map/psum | solution.py:58
  127.2 0.6 broadcast_multiply_fusion
  (5 shorter events, 0.1 us)
Async XLA Ops:
  23.2 7.6 %copy-start = (s32[16]{0:T(128)S(1)}, s32[16]{0:T(128)}, u32[]{:S(2)}) copy-start(s32[16]{0:T(128)} %param.12) | copy-start | bytes 196
  23.2 67.0 %all-to-all-start = ((f32[8,2,16,2560]{3,2,1,0:T(8,128)}), f32[8,2,16,2560]{3,2,1,0:T(8,128)S(1)}, u32[]{:S(2)}, u32[]{:S(2)}) async-start(f32[8,2,16,2560]{3,2,1,0:T(8,128)} %pad_maximum_fusion), calls=%async_computation | async-start | bytes 5242880 | tf_op jit(solution)/shard_map/all_to_all | solution.py:43
  30.7 59.6 %copy-start.1 = (s32[16]{0:T(128)S(1)}, s32[16]{0:T(128)}, u32[]{:S(2)}) copy-start(s32[16]{0:T(128)} %param.14) | copy-start | bytes 196
  30.7 59.6 %copy-start.2 = (s32[16]{0:T(128)S(1)}, s32[16]{0:T(128)}, u32[]{:S(2)}) copy-start(s32[16]{0:T(128)} %param.11) | copy-start | bytes 196
  30.7 59.6 %copy-start.3 = (s32[16]{0:T(128)S(1)}, s32[16]{0:T(128)}, u32[]{:S(2)}) copy-start(s32[16]{0:T(128)} %param.13) | copy-start | bytes 196
where the time goes:
time: 128 us
  waiting for transfers between devices  58.7 us (46%)
  blocking collectives  35.2 us (28%)
  between operations  9.63 us (8%)
  other arithmetic  7.82 us (6%)
  starting transfers between devices  7.53 us (6%)
  local copies, waits for them, and re-layouts  7.23 us (6%)
  matrix products  1.64 us (1%)
    all_to_all x1, waiting for transfers between devices, body(): lax.all_to_all(num_send, 'strip', split_axis=0, concat_axis=0, tiled=True)  58.7 us
    psum x1, blocking collectives, body(): column_sums = lax.psum(jnp.sum(stitched * stitched, axis=0), 'strip')  35.2 us
    all_to_all x1, starting transfers between devices, body(): lax.all_to_all(num_send, 'strip', split_axis=0, concat_axis=0, tiled=True)  7.53 us
    select_n x2, other arithmetic, body(): row_weight = jnp.where(inside, row_taper, 0.0)  2.63 us
  transfers between devices with their start and end apart: 1, of which 1 were waited for; matrix products, arithmetic and copies ran while one was open for 1% of the time, Pallas kernels for 0%

commit v1 on v0

--- a/solution.py
+++ b/solution.py
@@ -55,7 +55,7 @@
     denominator = jnp.einsum("fv,fu->vu", row_part, col_part, precision=lax.Precision.HIGHEST)
     numerator = jnp.sum(got_num, axis=(0, 1))
     stitched = numerator / jnp.maximum(denominator, 0.5)
-    column_sums = lax.psum(jnp.sum(stitched * stitched, axis=0), "strip")
+    column_sums = jnp.sum(lax.all_gather(jnp.sum(stitched * stitched, axis=0), "strip"), axis=0)
     return (stitched, column_sums / image_rows)
 
 

time: 128 us -> 124 us (0.969)
  blocking collectives: 35.2 us -> 30.5 us
    psum x1 -> x0, blocking collectives: 35.2 us -> none  [body(): column_sums = lax.psum(jnp.sum(stitched * stitched, axis=0), 'strip')]
    all_gather x0 -> x1, blocking collectives: none -> 30.5 us  [body(): lax.all_gather(jnp.sum(stitched * stitched, axis=0), 'strip')]
where the time goes in v1:
time: 124 us; the launch traced here: 123 us
  waiting for transfers between devices  58.7 us (47%)
  blocking collectives  30.5 us (25%)
  between operations  9.63 us (8%)
  other arithmetic  7.89 us (6%)
  starting transfers between devices  7.53 us (6%)
  local copies, waits for them, and re-layouts  7.23 us (6%)
  matrix products  1.64 us (1%)
    all_to_all x1, waiting for transfers between devices, body(): lax.all_to_all(num_send, 'strip', split_axis=0, concat_axis=0, tiled=True)  58.7 us
    all_gather x1, blocking collectives, body(): lax.all_gather(jnp.sum(stitched * stitched, axis=0), 'strip')  30.5 us
    all_to_all x1, starting transfers between devices, body(): lax.all_to_all(num_send, 'strip', split_axis=0, concat_axis=0, tiled=True)  7.53 us
    select_n x2, other arithmetic, body(): row_weight = jnp.where(inside, row_taper, 0.0)  2.63 us
  transfers between devices with their start and end apart: 1, of which 1 were waited for; matrix products, arithmetic and copies ran while one was open for 1% of the time, Pallas kernels for 0%

profile of v1, /device:TPU:0, one launch (start us, length us, event | category | flops | bytes accessed | tf_op | source)
XLA Modules:
  0.0 123.2 jit_solution(15755452113020551008)
XLA Ops:
  0.6 1.3 %fusion.47 = (s32[1]{0:T(128)}, s32[1]{0:T(128)}) fusion(s32[16]{0:T(128)} %param.15, s32[]{:T(128)S(6)} %select_n.50, s32[]{:T(128)S(6)} %select_n.54), kind=kLoop, calls=%fused_computation.69 | loop fusion | bytes 24 | tf_op jit(solution)/shard_map/dynamic_slice | solution.py:28
  4.6 0.1 sine_multiply_fusion
  5.9 1.4 %fusion.43 = (s32[1]{0:T(128)}, s32[1]{0:T(128)}, s32[1]{0:T(128)}, s32[1]{0:T(128)}) fusion(s32[16]{0:T(128)} %param.11, s32[]{:T(128)S(6)} %select_n.51, s32[]{:T(128)S(6)} %select_n.55, s32[16]{0:T(128)} %param.13), kind=kLoop, calls=%fused_computation.65 | loop fusion | bytes 40 | tf_op jit(solution)/shard_map/dynamic_slice | solution.py:40
  9.8 1.4 %fusion.45 = (s32[1]{0:T(128)}, s32[1]{0:T(128)}, s32[1]{0:T(128)}, s32[1]{0:T(128)}) fusion(s32[16]{0:T(128)} %param.14, s32[]{:T(128)S(6)} %select_n.51, s32[]{:T(128)S(6)} %select_n.55, s32[16]{0:T(128)} %param.12), kind=kLoop, calls=%fused_computation.67 | loop fusion | bytes 40 | tf_op jit(solution)/shard_map/dynamic_slice | solution.py:29
  12.5 1.2 %and_select_fusion = f32[64]{0:T(128)S(1)} fusion(s32[]{:T(128)} %bitcast.9, s32[]{:T(128)} %bitcast.8), kind=kLoop, calls=%fused_computation.55 | loop fusion | flops 512 | bytes 264 | tf_op jit(solution)/shard_map/jit(_where)/select_n | solution.py:30
  13.7 1.4 %and_select_fusion.1 = f32[64]{0:T(128)S(1)} fusion(s32[]{:T(128)} %bitcast.2, s32[]{:T(128)} %bitcast.1), kind=kLoop, calls=%fused_computation.56 | loop fusion | flops 512 | bytes 264 | tf_op jit(solution)/shard_map/jit(_where)/select_n | solution.py:30
  16.3 1.5 %fusion.1 = (f32[64,2560]{1,0:T(8,128)S(1)}, f32[64,2560]{1,0:T(8,128)S(1)}) fusion(f32[2,64,2560]{2,1,0:T(8,128)} %param.8, f32[2560]{0:T(1024)} %param.10, f32[64]{0:T(128)} %param.9, f32[2560]{0:T(1024)S(1)} %sine_multiply_fusion, f32[64]{0:T(128)S(1)} %and_select_fusion.1, f32[64]{0:T(128)S(1)} %and_select_fusion), kind=kLoop, calls=%fused_computation.12 | loop fusion | flops 1146880 | bytes 2642688 | tf_op jit(solution)/shard_map/mul | solution.py:36
  17.9 1.1 fusion.6
  19.0 0.1 broadcast.78.clone.1
  19.2 1.1 dynamic_update_slice.6
  20.3 0.1 broadcast.78.clone
  20.4 1.0 dynamic_update_slice.7
  21.4 1.7 %pad_maximum_fusion = f32[8,2,16,2560]{3,2,1,0:T(8,128)} fusion(f32[8,1,16,2560]{3,2,1,0:T(8,128)S(1)} %bitcast.16, f32[8,1,16,2560]{3,2,1,0:T(8,128)S(1)} %bitcast.17), kind=kLoop, calls=%fused_computation.7 | loop fusion | flops 655360 | bytes 5242880 | tf_op jit(solution)/shard_map/stack | solution.py:42
  23.2 0.0 copy-start
  23.2 7.5 %all-to-all-start = ((f32[8,2,16,2560]{3,2,1,0:T(8,128)}), f32[8,2,16,2560]{3,2,1,0:T(8,128)S(1)}, u32[]{:S(2)}, u32[]{:S(2)}) async-start(f32[8,2,16,2560]{3,2,1,0:T(8,128)} %pad_maximum_fusion), calls=%async_computation | async-start | bytes 5242880 | tf_op jit(solution)/shard_map/all_to_all | solution.py:43
  30.7 0.0 copy-start.1
  30.7 0.0 copy-start.2
  30.7 0.0 copy-start.3
  30.7 0.0 copy-done
  30.8 0.7 gather_fusion
  31.4 58.7 %all-to-all-done = f32[8,2,16,2560]{3,2,1,0:T(8,128)S(1)} async-done(((f32[8,2,16,2560]{3,2,1,0:T(8,128)}), f32[8,2,16,2560]{3,2,1,0:T(8,128)S(1)}, u32[]{:S(2)}, u32[]{:S(2)}) %all-to-all-start) | async-done | bytes 2621472 | tf_op jit(solution)/shard_map/all_to_all | solution.py:43
  90.2 0.1 reduce_sum.27
  90.3 0.0 copy-done.1
  90.3 0.0 copy-done.2
  90.3 0.0 copy-done.3
  90.3 1.6 %multiply_reduce_fusion = (f32[2560]{0:T(1024)S(1)}, f32[16,2560]{1,0:T(8,128)}) fusion(f32[16,2560]{1,0:T(8,128)S(1)} %reduce_sum.27, s32[16]{0:T(128)S(1)} %gather_fusion, s32[2560]{0:T(1024)S(1)} %iota_add_fusion, s32[16]{0:T(128)S(1)} %copy-done.1, s32[16]{0:T(128)S(1)} %copy-done.3, s32[16]{0:T(128)S(1)} %copy-done.2, s32[16]{0:T(128)S(1)} %iota_add_fusion.1), kind=kOutput, calls=%fused_computation.26 | convolution fusion | flops 8396544 | bytes 348480 | tf_op jit(solution)/shard_map/fv,fu->vu/dot_general | solution.py:55
  92.0 30.5 %all-gather.1 = f32[8,1,2560]{2,1,0:T(1,128)S(1)} all-gather(f32[1,1,2560]{2,1,0:T(1,128)S(1)} %reshape.61), channel_id=2, replica_groups=mesh['strip'=8,'col'=4] {'strip'}, dimensions={0}, use_global_device_ids=true | all-gather | bytes 92160 | tf_op jit(solution)/shard_map/all_gather | solution.py:58
  122.5 0.1 reduce_sum.29
  122.6 0.6 broadcast_multiply_fusion
  (6 shorter events, 0.1 us)
Async XLA Ops:
  23.2 7.6 %copy-start = (s32[16]{0:T(128)S(1)}, s32[16]{0:T(128)}, u32[]{:S(2)}) copy-start(s32[16]{0:T(128)} %param.12) | copy-start | bytes 196
  23.2 67.0 %all-to-all-start = ((f32[8,2,16,2560]{3,2,1,0:T(8,128)}), f32[8,2,16,2560]{3,2,1,0:T(8,128)S(1)}, u32[]{:S(2)}, u32[]{:S(2)}) async-start(f32[8,2,16,2560]{3,2,1,0:T(8,128)} %pad_maximum_fusion), calls=%async_computation | async-start | bytes 5242880 | tf_op jit(solution)/shard_map/all_to_all | solution.py:43
  30.7 59.6 %copy-start.1 = (s32[16]{0:T(128)S(1)}, s32[16]{0:T(128)}, u32[]{:S(2)}) copy-start(s32[16]{0:T(128)} %param.14) | copy-start | bytes 196
  30.7 59.6 %copy-start.2 = (s32[16]{0:T(128)S(1)}, s32[16]{0:T(128)}, u32[]{:S(2)}) copy-start(s32[16]{0:T(128)} %param.11) | copy-start | bytes 196
  30.7 59.6 %copy-start.3 = (s32[16]{0:T(128)S(1)}, s32[16]{0:T(128)}, u32[]{:S(2)}) copy-start(s32[16]{0:T(128)} %param.13) | copy-start | bytes 196
